TPU v7x, 32 devices: a whole 2x2x4 slice. The times are simulated.
32 devices in a mesh: order: 8 (over y, x, core), axial: 4 (over z).
Axes of the slice: x: 2, y: 2, z: 4, core: 2. Of those that a mesh axis runs over, the one named last changes fastest.
Arguments:
- coefficients: bfloat16 [4, 2, 1024, 8, 1024], P(None, None, 'order', 'axial'), may hold values from -0.005859375 to 0.005859375
- order_lists: int32 [1024], replicated, may hold values from 0 to 1023, as said below
- lengths: int32 [1024], replicated, may hold values from 128 to 1024, as said below
Outputs:
- advection: bfloat16 [3, 2, 1024, 8, 1024], P(None, None, 'order', 'axial')
Inputs may be any that keep to these rules, and one draw needn't show every extreme that they name: `order_lists`: a permutation of the orders 0 to 1023; the device with index j along order holds slots j * 128 to (j + 1) * 128 - 1 of coefficients and advection. lengths[m] minus (128 + ((1023 - m) * 768) // 1023) lies in 0 to 128.
All inputs are finite; a program needn't handle non-finite values.
Results may differ from a plain program's by a relative error of at most 0.0095.
Values may be sent and summed in bfloat16 or wider, within the bound.
A program may use at most 128 MiB of HBM per device.

v0:
```python
import math
import jax
import jax.numpy as jnp
from jax import lax
from jax.sharding import PartitionSpec as P

R = 1024


def with_halo(block, sides, width):
    for axis, dim in sides:
        count = lax.axis_size(axis)
        forward = [(i, i + 1) for i in range(count - 1)]
        forward.append((count - 1, 0))
        backward = [(target, source) for source, target in forward]
        low = lax.ppermute(
            lax.slice_in_dim(block, block.shape[dim] - width, None, axis=dim), axis, forward
        )
        high = lax.ppermute(lax.slice_in_dim(block, 0, width, axis=dim), axis, backward)
        block = jnp.concatenate([low, block, high], axis=dim)
    return block


def radial_tables(radius_count, mode_count):
    radius_ids = jnp.arange(radius_count, dtype=jnp.int32)
    mode_ids = jnp.arange(mode_count, dtype=jnp.int32)
    phases = mode_ids[None, :] * (2 * radius_ids[:, None] + 1) % (4 * radius_count)
    angles_rad = phases.astype(jnp.float32) * (math.pi / (2 * radius_count))
    synthesis = jnp.cos(angles_rad).astype(jnp.bfloat16)
    analysis = (jnp.cos(angles_rad.T) * math.sqrt(2.0 / radius_count)).astype(jnp.bfloat16)
    return (synthesis, analysis)


def azimuthal_tables(order_ids, point_count):
    points = jnp.arange(point_count, dtype=jnp.int32)
    phases = order_ids[..., None] * points % point_count
    angles_rad = phases.astype(jnp.float32) * (2.0 * math.pi / point_count)
    cosines = jnp.cos(angles_rad)
    sines = jnp.sin(angles_rad)
    weight = jnp.where(order_ids == 0, 1.0, 2.0).astype(jnp.float32)[..., None]
    forward = jnp.stack((weight * cosines, -weight * sines), axis=-3).astype(jnp.bfloat16)
    factor = math.sqrt(2.0 / point_count)
    inverse = jnp.stack((cosines * factor, -sines * factor), axis=-3).astype(jnp.bfloat16)
    return (forward, inverse)


def shards(coefficients, order_lists, lengths):
    field_count, part_count, slot_count, plane_count, mode_count = coefficients.shape
    order_count = order_lists.shape[0]
    point_count = 2 * order_count
    radius_count = R
    group_count = lax.axis_size("order")
    band_width = radius_count // group_count
    synthesis, analysis = radial_tables(radius_count, mode_count)
    owned_ids = lax.dynamic_slice_in_dim(
        order_lists, lax.axis_index("order") * slot_count, slot_count
    )
    catalog = jnp.arange(order_count, dtype=jnp.int32)
    own_lengths = jnp.sum(
        jnp.where(owned_ids[:, None] == catalog[None, :], lengths[None, :], 0), axis=1
    )
    retained = jnp.arange(mode_count, dtype=jnp.int32)[None, :] < own_lengths[:, None]
    masked = jnp.where(
        retained[None, None, :, None, :], coefficients, jnp.zeros((), coefficients.dtype)
    )
    radial = jnp.einsum("fcmzk,rk->frzcm", masked, synthesis, preferred_element_type=jnp.float32)
    radial = radial.astype(jnp.bfloat16).reshape(
        field_count, radius_count, plane_count * part_count * slot_count
    )
    forward, inverse = azimuthal_tables(order_lists.reshape(group_count, slot_count), point_count)
    received = lax.all_to_all(radial, "order", split_axis=1, concat_axis=2, tiled=True)
    item_count = received.shape[0]
    lattice = received.reshape(
        item_count, band_width, group_count, plane_count, part_count, slot_count
    )
    physical = jnp.einsum(
        "frizcm,icmj->fzrj", lattice, forward, preferred_element_type=jnp.float32
    ).astype(jnp.bfloat16)
    padded = with_halo(physical[:3], (("axial", 1),), 2)
    widened = padded.astype(jnp.float32)
    gradient = (
        8.0 * (widened[:, 3 : plane_count + 3] - widened[:, 1 : plane_count + 1])
        - (widened[:, 4 : plane_count + 4] - widened[:, 0:plane_count])
    ) / 12.0
    products = (physical[3].astype(jnp.float32)[None] * gradient).astype(jnp.bfloat16)
    spectral = jnp.einsum(
        "gzrj,icmj->grizcm", products, inverse, preferred_element_type=jnp.float32
    )
    spectral = spectral.astype(jnp.bfloat16).reshape(
        3, band_width, group_count * plane_count * part_count * slot_count
    )
    received = lax.all_to_all(spectral, "order", split_axis=2, concat_axis=1, tiled=True)
    item_count = received.shape[0]
    lattice = received.reshape(item_count, radius_count, plane_count, part_count, slot_count)
    result = jnp.einsum("grzcm,kr->gcmzk", lattice, analysis, preferred_element_type=jnp.float32)
    return jnp.where(retained[None, None, :, None, :], result, 0.0).astype(jnp.bfloat16)


def solution(mesh):
    placed = (P(None, None, "order", "axial", None), P(), P())
    return jax.shard_map(
        shards,
        mesh=mesh,
        in_specs=placed,
        out_specs=P(None, None, "order", "axial", None),
        check_vma=False,
    )
```

profile of v0, /device:TPU:0, one launch (start us, length us, event | category | flops | bytes accessed | tf_op | source)
XLA Modules:
  0.0 382.5 jit_solution(8791086650537149125)
XLA Ops:
  0.0 0.8 dynamic_slice.3
  0.8 0.9 select_reduce_fusion
  1.6 0.1 iota_compare_fusion.1
  1.8 0.2 copy.46
  2.0 9.3 %broadcast_select_fusion = bf16[4,2,128,2,1024]{4,3,2,1,0:T(2,128)(2,1)} fusion(bf16[4,2,128,2,1024]{4,3,2,1,0:T(2,128)(2,1)} %param.3, pred[128,1024]{1,0:T(8,128)(4,1)S(1)} %copy.46), kind=kLoop, calls=%fused_computation.22 | loop fusion | flops 2097152 | bytes 8519680 | tf_op jit(solution)/shard_map/jit(_where)/select_n | solution.py:63
  11.3 21.9 %convert_bitcast_fusion = bf16[4,1024,2,2,128]{1,4,2,3,0:T(8,128)(2,1)S(1)} fusion(bf16[4,2,128,2,1024]{4,3,2,1,0:T(2,128)(2,1)} %broadcast_select_fusion, s32[1024]{0:T(1024)S(1)} %multiply_add_fusion), kind=kOutput, calls=%fused_computation.51 | convolution fusion | flops 4312793088 | bytes 8392704 | tf_op jit(solution)/shard_map/fcmzk,rk->frzcm/dot_general | solution.py:66
  33.3 2.4 copy.48
  35.7 7.8 %copy.49 = bf16[4,1024,512]{2,0,1:T(4,128)(2,1)} copy(bf16[4,1024,512]{1,2,0:T(8,128)(2,1)} %bitcast.66) | data formatting | bytes 8388608 | tf_op jit(solution)/shard_map/reshape | solution.py:67
  43.5 5.6 %all-to-all-start = ((bf16[4,1024,512]{2,0,1:T(4,128)(2,1)}), bf16[4,1024,512]{2,0,1:T(4,128)(2,1)}, u32[]{:S(2)}, u32[]{:S(2)}) async-start(bf16[4,1024,512]{2,0,1:T(4,128)(2,1)} %copy.49), calls=%async_computation | async-start | bytes 8388608 | tf_op jit(solution)/shard_map/all_to_all | solution.py:71
  49.2 38.0 %multiply_convert_fusion.3 = (bf16[8,1,128,2048]{2,3,0,1:T(8,128)(2,1)}, bf16[8,1,128,2048]{2,3,0,1:T(8,128)(2,1)}, bf16[8,1,128,2048]{2,3,0,1:T(8,128)(2,1)}, bf16[8,1,128,2048]{2,3,0,1:T(8,128)(2,1)}) fusion(s32[8,128]{1,0:T(8,128)S(1)} %bitcast.71, f32[8,128]{1,0:T(8,128)S(1)} %get-tuple-element.9, f32[8,128]{1,0:T(8,128)S(1)} %get-tuple-element.10), kind=kLoop, calls=%fused_computation.18 | loop fusion | flops 48234496 | bytes 16789504 | tf_op jit(solution)/shard_map/convert.2
  87.2 11.1 %all-to-all-done = bf16[4,1024,512]{2,0,1:T(4,128)(2,1)} async-done(((bf16[4,1024,512]{2,0,1:T(4,128)(2,1)}), bf16[4,1024,512]{2,0,1:T(4,128)(2,1)}, u32[]{:S(2)}, u32[]{:S(2)}) %all-to-all-start) | async-done | bytes 4194336 | tf_op jit(solution)/shard_map/all_to_all | solution.py:71
  98.3 3.0 copy.50
  101.3 0.0 copy-start
  101.3 0.0 copy-start.1
  101.3 2.4 copy.51
  103.8 1.0 copy-done.1
  104.8 9.2 %fusion.38 = bf16[4,2,128,2048]{2,3,1,0:T(8,128)(2,1)S(1)} fusion(bf16[4,128,8,2,2,128]{5,2,4,3,1,0:T(8,128)(2,1)S(1)} %bitcast.70, bf16[8,1,128,2048]{2,3,0,1:T(8,128)(2,1)S(1)} %copy-done.1, bf16[8,1,128,2048]{2,3,0,1:T(8,128)(2,1)S(1)} %copy-done), kind=kOutput, calls=%fused_computation.60 | convolution fusion | flops 8608808960 | bytes 16777216 | tf_op jit(solution)/shard_map/frizcm,icmj->fzrj/dot_general | solution.py:76
  114.0 0.2 slice.24
  114.2 4.4 %collective-permute-start.1 = (bf16[3,2,128,2048]{2,3,1,0:T(8,128)(2,1)S(1)}, bf16[3,2,128,2048]{2,3,1,0:T(8,128)(2,1)S(1)}, u32[]{:S(2)}, u32[]{:S(2)}) collective-permute-start(bf16[3,2,128,2048]{2,3,1,0:T(8,128)(2,1)S(1)} %slice.24), channel_id=1, source_target_pairs={{1,0},{2,1},{3,2},{0,3},{5,4},{6,5},{7,6},{4,7},{9,8},{10,9},{11,1... | collective-permute-start | bytes 9437192 | tf_op jit(solution)/shard_map/ppermute | solution.py:19
  118.6 0.0 collective-permute-start
  118.6 1.5 multiply_bitcast_fusion
  120.1 67.0 %collective-permute-done.1 = bf16[3,2,128,2048]{2,3,1,0:T(8,128)(2,1)S(1)} collective-permute-done((bf16[3,2,128,2048]{2,3,1,0:T(8,128)(2,1)S(1)}, bf16[3,2,128,2048]{2,3,1,0:T(8,128)(2,1)S(1)}, u32[]{:S(2)}, u32[]{:S(2)}) %collective-permute-start.1) | collective-permute-done | bytes 3145760 | tf_op jit(solution)/shard_map/ppermute | solution.py:19
  187.1 64.2 %collective-permute-done = bf16[3,2,128,2048]{2,3,1,0:T(8,128)(2,1)S(1)} collective-permute-done((bf16[3,2,128,2048]{2,3,1,0:T(8,128)(2,1)S(1)}, bf16[3,2,128,2048]{2,3,1,0:T(8,128)(2,1)S(1)}, u32[]{:S(2)}, u32[]{:S(2)}) %collective-permute-start) | collective-permute-done | bytes 3145760 | tf_op jit(solution)/shard_map/ppermute | solution.py:16
  251.3 7.1 %maximum_convert_fusion = f32[3,6,128,2048]{2,3,1,0:T(8,128)} fusion(bf16[3,2,128,2048]{2,3,1,0:T(8,128)(2,1)S(1)} %collective-permute-done.1, bf16[3,2,128,2048]{2,3,1,0:T(8,128)(2,1)S(1)} %slice.24, bf16[3,2,128,2048]{2,3,1,0:T(8,128)(2,1)S(1)} %collective-permute-done), kind=kLoop, calls=%fused_computation.3 | loop fusion | flops 14155776 | bytes 28311552 | tf_op jit(solution)/shard_map/convert_element_type | solution.py:80
  258.4 18.2 %convert_bitcast_fusion.1 = bf16[3,128,8,2,2,128]{1,5,3,0,4,2:T(8,128)(2,1)S(1)} fusion(f32[2,128,2048]{1,2,0:T(8,128)} %multiply_bitcast_fusion, f32[3,6,128,2048]{2,3,1,0:T(8,128)} %maximum_convert_fusion, bf16[8,1,128,2048]{2,3,0,1:T(8,128)(2,1)} %get-tuple-element.7, bf16[8,1,128,2048]{2,3,0,1:T(8,128)(2,1)} %get-tuple-element.5), kind=kOutput, calls=%fused_computation.63 | convolution fusion | flops 6457655296 | bytes 38797312 | tf_op jit(solution)/shard_map/gzrj,icmj->grizcm/dot_general | solution.py:86
  276.6 0.2 copy.55
  276.8 20.0 %copy.56 = bf16[3,128,4096]{1,0,2:T(4,128)(2,1)S(1)} copy(bf16[3,128,4096]{1,2,0:T(8,128)(2,1)S(1)} %bitcast.68) | data formatting | bytes 6291456 | tf_op jit(solution)/shard_map/reshape | solution.py:89
  296.8 53.8 %all_to_all.30 = bf16[3,128,4096]{1,0,2:T(4,128)(2,1)S(1)} all-to-all(bf16[3,128,4096]{1,0,2:T(4,128)(2,1)S(1)} %copy.56), channel_id=1, replica_groups=mesh['order'=8,'axial'=4] {'order'}, dimensions={2} | all-to-all | bytes 6291456 | tf_op jit(solution)/shard_map/all_to_all | solution.py:92
  350.6 2.6 copy.83
  353.2 3.3 reshape.125
  356.5 20.2 %fusion.15 = bf16[3,2,128,2,1024]{2,4,1,3,0:T(8,128)(2,1)S(1)} fusion(pred[128,1024]{0,1:T(8,128)(4,1)S(1)} %iota_compare_fusion.1, bf16[3,1024,2,2,128]{1,4,3,2,0:T(8,128)(2,1)} %reshape.125, s32[1024]{0:T(1024)S(1)} %multiply_add_fusion), kind=kOutput, calls=%fused_computation.30 | convolution fusion | flops 3241148416 | bytes 6426624 | tf_op jit(solution)/shard_map/grzcm,kr->gcmzk/dot_general | solution.py:95
  376.7 5.6 %copy.59 = bf16[3,2,128,2,1024]{4,3,2,1,0:T(2,128)(2,1)} copy(bf16[3,2,128,2,1024]{2,4,1,3,0:T(8,128)(2,1)S(1)} %fusion.15) | data formatting | bytes 6291456 | tf_op jit(solution)/shard_map/convert_element_type | solution.py:96
  (5 shorter events, 0.0 us)
Async XLA Ops:
  43.5 5.6 %copy-start.2 = (s32[1024]{0:T(1024)S(1)}, s32[1024]{0:T(1024)}, u32[]{:S(2)}) copy-start(s32[1024]{0:T(1024)} %param.4) | copy-start | bytes 12292
  43.5 54.8 %all-to-all-start = ((bf16[4,1024,512]{2,0,1:T(4,128)(2,1)}), bf16[4,1024,512]{2,0,1:T(4,128)(2,1)}, u32[]{:S(2)}, u32[]{:S(2)}) async-start(bf16[4,1024,512]{2,0,1:T(4,128)(2,1)} %copy.49), calls=%async_computation | async-start | bytes 8388608 | tf_op jit(solution)/shard_map/all_to_all | solution.py:71
  101.3 2.4 copy-start
  101.3 3.5 copy-start.1
  114.2 72.9 %collective-permute-start.1 = (bf16[3,2,128,2048]{2,3,1,0:T(8,128)(2,1)S(1)}, bf16[3,2,128,2048]{2,3,1,0:T(8,128)(2,1)S(1)}, u32[]{:S(2)}, u32[]{:S(2)}) collective-permute-start(bf16[3,2,128,2048]{2,3,1,0:T(8,128)(2,1)S(1)} %slice.24), channel_id=1, source_target_pairs={{1,0},{2,1},{3,2},{0,3},{5,4},{6,5},{7,6},{4,7},{9,8},{10,9},{11,1... | collective-permute-start | bytes 9437192 | tf_op jit(solution)/shard_map/ppermute | solution.py:19
  118.6 132.7 %collective-permute-start = (bf16[3,2,128,2048]{2,3,1,0:T(8,128)(2,1)S(1)}, bf16[3,2,128,2048]{2,3,1,0:T(8,128)(2,1)S(1)}, u32[]{:S(2)}, u32[]{:S(2)}) collective-permute-start(bf16[3,2,128,2048]{2,3,1,0:T(8,128)(2,1)S(1)} %slice.24), channel_id=1, source_target_pairs={{0,1},{1,2},{2,3},{3,0},{4,5},{5,6},{6,7},{7,4},{8,9},{9,10},{10,1... | collective-permute-start | bytes 9437192 | tf_op jit(solution)/shard_map/ppermute | solution.py:16
where the time goes:
time: 388 us; the launch traced here: 382 us
  waiting for transfers between devices  142 us (37%)
  matrix products  69.5 us (18%)
  other arithmetic  56.9 us (15%)
  blocking collectives  53.8 us (14%)
  local copies, waits for them, and re-layouts  49.6 us (13%)
  starting transfers between devices  9.99 us (3%)
    ppermute x1, waiting for transfers between devices, with_halo(): lax.ppermute(lax.slice_in_dim(block, 0, width, axis=dim), axis, backward)  67 us
    ppermute x1, waiting for transfers between devices, with_halo(): lax.ppermute(lax.slice_in_dim(block, block.shape[dim] - width, None, axis...  64.2 us
    all_to_all x1, blocking collectives, shards(): lax.all_to_all(spectral, 'order', split_axis=2, concat_axis=1, tiled=True)  53.8 us
    another operation x1, other arithmetic  38 us
    dot_general x1, matrix products, shards(): jnp.einsum('fcmzk,rk->frzcm', masked, synthesis, preferred_element_type=j...  21.9 us
    dot_general x1, matrix products, shards(): jnp.einsum('grzcm,kr->gcmzk', lattice, analysis, preferred_element_type=j...  20.2 us
    reshape x1, local copies, waits for them, and re-layouts, shards(): spectral.astype(jnp.bfloat16)  20 us
    dot_general x1, matrix products, shards(): jnp.einsum('gzrj,icmj->grizcm', products, inverse, preferred_element_type...  18.2 us
  transfers between devices with their start and end apart: 3, of which 3 were waited for; matrix products, arithmetic and copies ran while one was open for 10% of the time, Pallas kernels for 0%

commit v1 on v0

--- a/solution.py
+++ b/solution.py
@@ -89,7 +89,9 @@
     spectral = spectral.astype(jnp.bfloat16).reshape(
         3, band_width, group_count * plane_count * part_count * slot_count
     )
-    received = lax.all_to_all(spectral, "order", split_axis=2, concat_axis=1, tiled=True)
+    cells = jnp.split(spectral, lax.axis_size("order"), axis=2)
+    incoming = lax.all_to_all(jnp.stack(cells), "order", 0, 0)
+    received = jnp.concatenate(incoming, axis=1)
     item_count = received.shape[0]
     lattice = received.reshape(item_count, radius_count, plane_count, part_count, slot_count)
     result = jnp.einsum("grzcm,kr->gcmzk", lattice, analysis, preferred_element_type=jnp.float32)

time: 388 us -> 357 us (0.920)
  local copies, waits for them, and re-layouts: 49.6 us -> 29.5 us
  blocking collectives: 53.8 us -> 42.8 us
    reshape x2 -> x1, local copies, waits for them, and re-layouts: 23.3 us -> 2.03 us  [shards(): received = jnp.concatenate(incoming, axis=1)]
    all_to_all x1, blocking collectives: 53.8 us -> 42.8 us  [shards(): incoming = lax.all_to_all(jnp.stack(cells), 'order', 0, 0)]
  transfers between devices with their start and end apart: 3 -> 3, of which waited for: 3 -> 3; matrix products, arithmetic and copies ran while one was open for 10% -> 11% of each run, Pallas kernels for 0% -> 0%
where the time goes in v1:
time: 357 us; the launch traced here: 351 us
  waiting for transfers between devices  142 us (40%)
  matrix products  69.7 us (20%)
  other arithmetic  56.7 us (16%)
  blocking collectives  42.8 us (12%)
  local copies, waits for them, and re-layouts  29.5 us (8%)
  starting transfers between devices  9.97 us (3%)
    ppermute x1, waiting for transfers between devices, with_halo(): lax.ppermute(lax.slice_in_dim(block, 0, width, axis=dim), axis, backward)  67 us
    ppermute x1, waiting for transfers between devices, with_halo(): lax.ppermute(lax.slice_in_dim(block, block.shape[dim] - width, None, axis...  64.2 us
    all_to_all x1, blocking collectives, shards(): incoming = lax.all_to_all(jnp.stack(cells), 'order', 0, 0)  42.8 us
    another operation x1, other arithmetic  38 us
    dot_general x1, matrix products, shards(): jnp.einsum('fcmzk,rk->frzcm', masked, synthesis, preferred_element_type=j...  22.2 us
    dot_general x1, matrix products, shards(): jnp.einsum('grzcm,kr->gcmzk', lattice, analysis, preferred_element_type=j...  20 us
    dot_general x1, matrix products, shards(): jnp.einsum('gzrj,icmj->grizcm', products, inverse, preferred_element_type...  18.2 us
    all_to_all x1, waiting for transfers between devices, shards(): lax.all_to_all(radial, 'order', split_axis=1, concat_axis=2, tiled=True)  11.1 us
  transfers between devices with their start and end apart: 3, of which 3 were waited for; matrix products, arithmetic and copies ran while one was open for 11% of the time, Pallas kernels for 0%

profile of v1, /device:TPU:0, one launch (start us, length us, event | category | flops | bytes accessed | tf_op | source)
XLA Modules:
  0.0 351.4 jit_solution(5074464116270954435)
XLA Ops:
  0.0 0.8 dynamic_slice.3
  0.8 0.9 select_reduce_fusion
  1.6 0.1 iota_compare_fusion.1
  1.8 0.2 copy.44
  2.0 9.3 %broadcast_select_fusion = bf16[4,2,128,2,1024]{4,3,2,1,0:T(2,128)(2,1)} fusion(bf16[4,2,128,2,1024]{4,3,2,1,0:T(2,128)(2,1)} %param.3, pred[128,1024]{1,0:T(8,128)(4,1)S(1)} %copy.44), kind=kLoop, calls=%fused_computation.22 | loop fusion | flops 2097152 | bytes 8519680 | tf_op jit(solution)/shard_map/jit(_where)/select_n | solution.py:63
  11.3 22.2 %convert_bitcast_fusion = bf16[4,1024,2,2,128]{1,4,2,3,0:T(8,128)(2,1)S(1)} fusion(bf16[4,2,128,2,1024]{4,3,2,1,0:T(2,128)(2,1)} %broadcast_select_fusion, s32[1024]{0:T(1024)S(1)} %multiply_add_fusion), kind=kOutput, calls=%fused_computation.51 | convolution fusion | flops 4312793088 | bytes 8392704 | tf_op jit(solution)/shard_map/fcmzk,rk->frzcm/dot_general | solution.py:66
  33.6 2.4 copy.46
  36.0 7.8 %copy.47 = bf16[4,1024,512]{2,0,1:T(4,128)(2,1)} copy(bf16[4,1024,512]{1,2,0:T(8,128)(2,1)} %bitcast.94) | data formatting | bytes 8388608 | tf_op jit(solution)/shard_map/reshape | solution.py:67
  43.8 5.5 %all-to-all-start = ((bf16[4,1024,512]{2,0,1:T(4,128)(2,1)}), bf16[4,1024,512]{2,0,1:T(4,128)(2,1)}, u32[]{:S(2)}, u32[]{:S(2)}) async-start(bf16[4,1024,512]{2,0,1:T(4,128)(2,1)} %copy.47), calls=%async_computation | async-start | bytes 8388608 | tf_op jit(solution)/shard_map/all_to_all | solution.py:71
  49.4 38.0 %multiply_convert_fusion.3 = (bf16[8,1,128,2048]{2,3,0,1:T(8,128)(2,1)}, bf16[8,1,128,2048]{2,3,0,1:T(8,128)(2,1)}, bf16[8,1,128,2048]{2,3,0,1:T(8,128)(2,1)}, bf16[8,1,128,2048]{2,3,0,1:T(8,128)(2,1)}) fusion(s32[8,128]{1,0:T(8,128)S(1)} %bitcast.106, f32[8,128]{1,0:T(8,128)S(1)} %get-tuple-element.9, f32[8,128]{1,0:T(8,128)S(1)} %get-tuple-element.10), kind=kLoop, calls=%fused_computation.18 | loop fusion | flops 48234496 | bytes 16789504 | tf_op jit(solution)/shard_map/convert.2
  87.4 11.1 %all-to-all-done = bf16[4,1024,512]{2,0,1:T(4,128)(2,1)} async-done(((bf16[4,1024,512]{2,0,1:T(4,128)(2,1)}), bf16[4,1024,512]{2,0,1:T(4,128)(2,1)}, u32[]{:S(2)}, u32[]{:S(2)}) %all-to-all-start) | async-done | bytes 4194336 | tf_op jit(solution)/shard_map/all_to_all | solution.py:71
  98.5 3.0 copy.48
  101.6 2.4 copy.49
  104.0 1.0 copy-done.1
  105.0 9.2 %fusion.38 = bf16[4,2,128,2048]{2,3,1,0:T(8,128)(2,1)S(1)} fusion(bf16[4,128,8,2,2,128]{5,2,4,3,1,0:T(8,128)(2,1)S(1)} %bitcast.105, bf16[8,1,128,2048]{2,3,0,1:T(8,128)(2,1)S(1)} %copy-done.1, bf16[8,1,128,2048]{2,3,0,1:T(8,128)(2,1)S(1)} %copy-done), kind=kOutput, calls=%fused_computation.60 | convolution fusion | flops 8608808960 | bytes 16777216 | tf_op jit(solution)/shard_map/frizcm,icmj->fzrj/dot_general | solution.py:76
  114.3 0.2 slice.24
  114.5 4.4 %collective-permute-start.1 = (bf16[3,2,128,2048]{2,3,1,0:T(8,128)(2,1)S(1)}, bf16[3,2,128,2048]{2,3,1,0:T(8,128)(2,1)S(1)}, u32[]{:S(2)}, u32[]{:S(2)}) collective-permute-start(bf16[3,2,128,2048]{2,3,1,0:T(8,128)(2,1)S(1)} %slice.24), channel_id=1, source_target_pairs={{1,0},{2,1},{3,2},{0,3},{5,4},{6,5},{7,6},{4,7},{9,8},{10,9},{11,1... | collective-permute-start | bytes 9437192 | tf_op jit(solution)/shard_map/ppermute | solution.py:19
  118.9 1.5 multiply_bitcast_fusion
  120.4 67.0 %collective-permute-done.1 = bf16[3,2,128,2048]{2,3,1,0:T(8,128)(2,1)S(1)} collective-permute-done((bf16[3,2,128,2048]{2,3,1,0:T(8,128)(2,1)S(1)}, bf16[3,2,128,2048]{2,3,1,0:T(8,128)(2,1)S(1)}, u32[]{:S(2)}, u32[]{:S(2)}) %collective-permute-start.1) | collective-permute-done | bytes 3145760 | tf_op jit(solution)/shard_map/ppermute | solution.py:19
  187.4 64.2 %collective-permute-done = bf16[3,2,128,2048]{2,3,1,0:T(8,128)(2,1)S(1)} collective-permute-done((bf16[3,2,128,2048]{2,3,1,0:T(8,128)(2,1)S(1)}, bf16[3,2,128,2048]{2,3,1,0:T(8,128)(2,1)S(1)}, u32[]{:S(2)}, u32[]{:S(2)}) %collective-permute-start) | collective-permute-done | bytes 3145760 | tf_op jit(solution)/shard_map/ppermute | solution.py:16
  251.6 6.9 %maximum_convert_fusion = f32[3,6,128,2048]{2,3,1,0:T(8,128)} fusion(bf16[3,2,128,2048]{2,3,1,0:T(8,128)(2,1)S(1)} %collective-permute-done.1, bf16[3,2,128,2048]{2,3,1,0:T(8,128)(2,1)S(1)} %slice.24, bf16[3,2,128,2048]{2,3,1,0:T(8,128)(2,1)S(1)} %collective-permute-done), kind=kLoop, calls=%fused_computation.3 | loop fusion | flops 14155776 | bytes 28311552 | tf_op jit(solution)/shard_map/convert_element_type | solution.py:80
  258.5 18.2 %convert_bitcast_fusion.1 = bf16[3,128,8,2,2,128]{1,5,3,0,4,2:T(8,128)(2,1)S(1)} fusion(f32[2,128,2048]{1,2,0:T(8,128)} %multiply_bitcast_fusion, f32[3,6,128,2048]{2,3,1,0:T(8,128)} %maximum_convert_fusion, bf16[8,1,128,2048]{2,3,0,1:T(8,128)(2,1)} %get-tuple-element.7, bf16[8,1,128,2048]{2,3,0,1:T(8,128)(2,1)} %get-tuple-element.5), kind=kOutput, calls=%fused_computation.62 | convolution fusion | flops 6457655296 | bytes 38797312 | tf_op jit(solution)/shard_map/gzrj,icmj->grizcm/dot_general | solution.py:86
  276.7 0.2 copy.53
  276.9 0.1 fusion.71
  277.0 0.1 fusion.70
  277.0 0.1 fusion.69
  277.1 0.1 fusion.68
  277.4 42.8 %all_to_all.20 = bf16[8,3,128,512]{2,3,1,0:T(8,128)(2,1)S(1)} all-to-all(bf16[8,3,128,512]{2,3,1,0:T(8,128)(2,1)S(1)} %fusion.65), channel_id=1, replica_groups=mesh['order'=8,'axial'=4] {'order'}, dimensions={0} | all-to-all | bytes 6291456 | tf_op jit(solution)/shard_map/all_to_all | solution.py:93
  320.1 2.0 copy.54
  322.2 3.3 reshape_reshape.3
  325.5 20.0 %fusion.15 = bf16[3,2,128,2,1024]{2,4,1,3,0:T(8,128)(2,1)S(1)} fusion(pred[128,1024]{0,1:T(8,128)(4,1)S(1)} %iota_compare_fusion.1, bf16[3,1024,2,2,128]{1,4,3,2,0:T(8,128)(2,1)} %reshape_reshape.3, s32[1024]{0:T(1024)S(1)} %multiply_add_fusion), kind=kOutput, calls=%fused_computation.30 | convolution fusion | flops 3241148416 | bytes 6426624 | tf_op jit(solution)/shard_map/grzcm,kr->gcmzk/dot_general | solution.py:97
  345.5 5.6 %copy.56 = bf16[3,2,128,2,1024]{4,3,2,1,0:T(2,128)(2,1)} copy(bf16[3,2,128,2,1024]{2,4,1,3,0:T(8,128)(2,1)S(1)} %fusion.15) | data formatting | bytes 6291456 | tf_op jit(solution)/shard_map/convert_element_type | solution.py:98
  (12 shorter events, 0.2 us)
Async XLA Ops:
  43.8 5.6 %copy-start.2 = (s32[1024]{0:T(1024)S(1)}, s32[1024]{0:T(1024)}, u32[]{:S(2)}) copy-start(s32[1024]{0:T(1024)} %param.4) | copy-start | bytes 12292
  43.8 54.7 %all-to-all-start = ((bf16[4,1024,512]{2,0,1:T(4,128)(2,1)}), bf16[4,1024,512]{2,0,1:T(4,128)(2,1)}, u32[]{:S(2)}, u32[]{:S(2)}) async-start(bf16[4,1024,512]{2,0,1:T(4,128)(2,1)} %copy.47), calls=%async_computation | async-start | bytes 8388608 | tf_op jit(solution)/shard_map/all_to_all | solution.py:71
  101.6 2.4 copy-start
  101.6 3.5 copy-start.1
  114.5 72.9 %collective-permute-start.1 = (bf16[3,2,128,2048]{2,3,1,0:T(8,128)(2,1)S(1)}, bf16[3,2,128,2048]{2,3,1,0:T(8,128)(2,1)S(1)}, u32[]{:S(2)}, u32[]{:S(2)}) collective-permute-start(bf16[3,2,128,2048]{2,3,1,0:T(8,128)(2,1)S(1)} %slice.24), channel_id=1, source_target_pairs={{1,0},{2,1},{3,2},{0,3},{5,4},{6,5},{7,6},{4,7},{9,8},{10,9},{11,1... | collective-permute-start | bytes 9437192 | tf_op jit(solution)/shard_map/ppermute | solution.py:19
  118.9 132.7 %collective-permute-start = (bf16[3,2,128,2048]{2,3,1,0:T(8,128)(2,1)S(1)}, bf16[3,2,128,2048]{2,3,1,0:T(8,128)(2,1)S(1)}, u32[]{:S(2)}, u32[]{:S(2)}) collective-permute-start(bf16[3,2,128,2048]{2,3,1,0:T(8,128)(2,1)S(1)} %slice.24), channel_id=1, source_target_pairs={{0,1},{1,2},{2,3},{3,0},{4,5},{5,6},{6,7},{7,4},{8,9},{9,10},{10,1... | collective-permute-start | bytes 9437192 | tf_op jit(solution)/shard_map/ppermute | solution.py:16
